TPU v7x, 128 devices: a whole 4x4x4 slice. The times are simulated.
128 devices in a mesh: batch: 1, seq_hi: 16 (over z, y), seq: 8 (over x, core).
Axes of the slice: x: 4, y: 4, z: 4, core: 2. Of those that a mesh axis runs over, the one named last changes fastest.
Arguments:
- x_seq: bfloat16 [32, 16384, 64], P('batch', ('seq_hi', 'seq'))
- w_f0: bfloat16 [3, 10, 64, 64], replicated
- w_f1: bfloat16 [3, 10, 64, 64], replicated
- w_g0: bfloat16 [3, 10, 64, 64], replicated
- w_g1: bfloat16 [3, 10, 64, 64], replicated
- w_res: bfloat16 [3, 10, 64, 64], replicated
- w_skip: bfloat16 [3, 10, 64, 64], replicated
Outputs:
- output 1: float32 [32, 16384, 64], P('batch', ('seq_hi', 'seq'))
- output 2: float32 [32, 16384, 64], P('batch', ('seq_hi', 'seq'))
All inputs are finite; a program needn't handle non-finite values.
Results may differ from a plain program's by a relative error of at most 0.0081759.
Values are sent between devices in bfloat16 or wider.
A program may use at most 1 GiB of HBM per device.

v0:
```python
import jax
import jax.numpy as jnp
from jax import lax
from jax.sharding import PartitionSpec as P

SEQ_AXES = ("seq_hi", "seq")


def move_right(block, hops, n_shards):
    if hops >= n_shards:
        return jnp.zeros_like(block)
    return lax.ppermute(block, SEQ_AXES, perm=[(source, source + hops) for source in range(n_shards - hops)])


def delay_rows(current, dilation, n_shards):
    local_len = current.shape[1]
    hops, rest = divmod(dilation, local_len)
    pieces = []
    if rest > 0:
        pieces.append(move_right(current[:, local_len - rest:], hops + 1, n_shards))
    if hops > 0:
        pieces.append(move_right(current[:, :local_len - rest], hops, n_shards))
    else:
        pieces.append(current[:, :local_len - rest])
    if len(pieces) == 1:
        return pieces[0]
    return jnp.concatenate(pieces, axis=1)


def gated_layer(residual, skip_acc, current, delayed, w_cur, w_del, w_out):
    chans = residual.shape[-1]
    gates = jnp.einsum("bsc,cd->bsd", current, w_cur, preferred_element_type=jnp.float32) + jnp.einsum("bsc,cd->bsd", delayed, w_del, preferred_element_type=jnp.float32)
    activated = (jnp.tanh(gates[..., :chans]) * jax.nn.sigmoid(gates[..., chans:])).astype(jnp.bfloat16)
    mixed = jnp.einsum("bsc,cd->bsd", activated, w_out, preferred_element_type=jnp.float32)
    return residual + mixed[..., :chans], skip_acc + mixed[..., chans:]


def solution(mesh):
    n_shards = mesh.shape["seq_hi"] * mesh.shape["seq"]
    seq_spec = P("batch", SEQ_AXES, None)

    def local_stack(x_loc, w_f0, w_f1, w_g0, w_g1, w_res, w_skip):
        n_rep, n_cyc = w_f0.shape[0], w_f0.shape[1]
        w_cur = jnp.concatenate([w_f1, w_g1], axis=-1)
        w_del = jnp.concatenate([w_f0, w_g0], axis=-1)
        w_out = jnp.concatenate([w_res, w_skip], axis=-1)
        residual = x_loc.astype(jnp.float32)
        skip_acc = jnp.zeros(x_loc.shape[:2] + (w_skip.shape[-1],), jnp.float32)
        for rep_idx in range(n_rep):
            for cyc_idx in range(n_cyc):
                current = residual.astype(jnp.bfloat16)
                delayed = delay_rows(current, 2 ** cyc_idx, n_shards)
                residual, skip_acc = gated_layer(residual, skip_acc, current, delayed, w_cur[rep_idx, cyc_idx], w_del[rep_idx, cyc_idx], w_out[rep_idx, cyc_idx])
        return residual, skip_acc

    return jax.shard_map(local_stack, mesh=mesh, in_specs=(seq_spec, P(), P(), P(), P(), P(), P()), out_specs=(seq_spec, seq_spec), check_vma=False)
```

profile of v0, /device:TPU:96, one launch (start us, length us, event | category | flops | bytes accessed | tf_op | source)
XLA Modules:
  0.0 525.7 jit_solution(18375384368297980543)
XLA Ops:
  39.1 12.2 %collective-permute-done.2 = bf16[32,4,64]{1,2,0:T(8,128)(2,1)S(1)} collective-permute-done((bf16[32,4,64]{1,2,0:T(8,128)(2,1)S(1)}, bf16[32,4,64]{1,2,0:T(8,128)(2,1)S(1)}, u32[]{:S(2)}, u32[]{:S(2)}) %collective-permute-start.2) | collective-permute-done | bytes 16416 | tf_op jit(solution)/shard_map/ppermute | solution.py:12
  55.5 12.2 %collective-permute-done.3 = bf16[32,8,64]{1,2,0:T(8,128)(2,1)S(1)} collective-permute-done((bf16[32,8,64]{1,2,0:T(8,128)(2,1)S(1)}, bf16[32,8,64]{1,2,0:T(8,128)(2,1)S(1)}, u32[]{:S(2)}, u32[]{:S(2)}) %collective-permute-start.3) | collective-permute-done | bytes 32800 | tf_op jit(solution)/shard_map/ppermute | solution.py:12
  73.0 12.2 %collective-permute-done.4 = bf16[32,16,64]{1,2,0:T(8,128)(2,1)S(1)} collective-permute-done((bf16[32,16,64]{1,2,0:T(8,128)(2,1)S(1)}, bf16[32,16,64]{1,2,0:T(8,128)(2,1)S(1)}, u32[]{:S(2)}, u32[]{:S(2)}) %collective-permute-start.4) | collective-permute-done | bytes 65568 | tf_op jit(solution)/shard_map/ppermute | solution.py:12
  106.9 12.2 %collective-permute-done.6 = bf16[32,64,64]{1,2,0:T(8,128)(2,1)S(1)} collective-permute-done((bf16[32,64,64]{1,2,0:T(8,128)(2,1)S(1)}, bf16[32,64,64]{1,2,0:T(8,128)(2,1)S(1)}, u32[]{:S(2)}, u32[]{:S(2)}) %collective-permute-start.6) | collective-permute-done | bytes 262176 | tf_op jit(solution)/shard_map/ppermute | solution.py:12
  123.0 12.2 %collective-permute-done.7 = bf16[32,128,64]{1,2,0:T(8,128)(2,1)S(1)} collective-permute-done((bf16[32,128,64]{1,2,0:T(8,128)(2,1)S(1)}, bf16[32,128,64]{1,2,0:T(8,128)(2,1)S(1)}, u32[]{:S(2)}, u32[]{:S(2)}) %collective-permute-start.7) | collective-permute-done | bytes 524320 | tf_op jit(solution)/shard_map/ppermute | solution.py:12
  140.3 12.8 %collective-permute-done.8 = bf16[32,128,64]{1,2,0:T(8,128)(2,1)S(1)} collective-permute-done((bf16[32,128,64]{1,2,0:T(8,128)(2,1)S(1)}, bf16[32,128,64]{1,2,0:T(8,128)(2,1)S(1)}, u32[]{:S(2)}, u32[]{:S(2)}) %collective-permute-start.8) | collective-permute-done | bytes 524320 | tf_op jit(solution)/shard_map/ppermute | solution.py:12
  157.0 13.1 %collective-permute-done.9 = bf16[32,128,64]{1,2,0:T(8,128)(2,1)S(1)} collective-permute-done((bf16[32,128,64]{1,2,0:T(8,128)(2,1)S(1)}, bf16[32,128,64]{1,2,0:T(8,128)(2,1)S(1)}, u32[]{:S(2)}, u32[]{:S(2)}) %collective-permute-start.9) | collective-permute-done | bytes 524320 | tf_op jit(solution)/shard_map/ppermute | solution.py:12
  175.3 12.2 %collective-permute-done.10 = bf16[32,1,64]{1,2,0:T(8,128)(2,1)S(1)} collective-permute-done((bf16[32,1,64]{1,2,0:T(8,128)(2,1)S(1)}, bf16[32,1,64]{1,2,0:T(8,128)(2,1)S(1)}, u32[]{:S(2)}, u32[]{:S(2)}) %collective-permute-start.10) | collective-permute-done | bytes 4128 | tf_op jit(solution)/shard_map/ppermute | solution.py:12
  209.2 12.2 %collective-permute-done.12 = bf16[32,4,64]{1,2,0:T(8,128)(2,1)S(1)} collective-permute-done((bf16[32,4,64]{1,2,0:T(8,128)(2,1)S(1)}, bf16[32,4,64]{1,2,0:T(8,128)(2,1)S(1)}, u32[]{:S(2)}, u32[]{:S(2)}) %collective-permute-start.12) | collective-permute-done | bytes 16416 | tf_op jit(solution)/shard_map/ppermute | solution.py:12
  225.6 12.2 %collective-permute-done.13 = bf16[32,8,64]{1,2,0:T(8,128)(2,1)S(1)} collective-permute-done((bf16[32,8,64]{1,2,0:T(8,128)(2,1)S(1)}, bf16[32,8,64]{1,2,0:T(8,128)(2,1)S(1)}, u32[]{:S(2)}, u32[]{:S(2)}) %collective-permute-start.13) | collective-permute-done | bytes 32800 | tf_op jit(solution)/shard_map/ppermute | solution.py:12
  243.1 12.2 %collective-permute-done.14 = bf16[32,16,64]{1,2,0:T(8,128)(2,1)S(1)} collective-permute-done((bf16[32,16,64]{1,2,0:T(8,128)(2,1)S(1)}, bf16[32,16,64]{1,2,0:T(8,128)(2,1)S(1)}, u32[]{:S(2)}, u32[]{:S(2)}) %collective-permute-start.14) | collective-permute-done | bytes 65568 | tf_op jit(solution)/shard_map/ppermute | solution.py:12
  259.4 12.2 %collective-permute-done.15 = bf16[32,32,64]{1,2,0:T(8,128)(2,1)S(1)} collective-permute-done((bf16[32,32,64]{1,2,0:T(8,128)(2,1)S(1)}, bf16[32,32,64]{1,2,0:T(8,128)(2,1)S(1)}, u32[]{:S(2)}, u32[]{:S(2)}) %collective-permute-start.15) | collective-permute-done | bytes 131104 | tf_op jit(solution)/shard_map/ppermute | solution.py:12
  293.2 12.2 %collective-permute-done.17 = bf16[32,128,64]{1,2,0:T(8,128)(2,1)S(1)} collective-permute-done((bf16[32,128,64]{1,2,0:T(8,128)(2,1)S(1)}, bf16[32,128,64]{1,2,0:T(8,128)(2,1)S(1)}, u32[]{:S(2)}, u32[]{:S(2)}) %collective-permute-start.17) | collective-permute-done | bytes 524320 | tf_op jit(solution)/shard_map/ppermute | solution.py:12
  310.4 12.8 %collective-permute-done.18 = bf16[32,128,64]{1,2,0:T(8,128)(2,1)S(1)} collective-permute-done((bf16[32,128,64]{1,2,0:T(8,128)(2,1)S(1)}, bf16[32,128,64]{1,2,0:T(8,128)(2,1)S(1)}, u32[]{:S(2)}, u32[]{:S(2)}) %collective-permute-start.18) | collective-permute-done | bytes 524320 | tf_op jit(solution)/shard_map/ppermute | solution.py:12
  327.1 13.1 %collective-permute-done.19 = bf16[32,128,64]{1,2,0:T(8,128)(2,1)S(1)} collective-permute-done((bf16[32,128,64]{1,2,0:T(8,128)(2,1)S(1)}, bf16[32,128,64]{1,2,0:T(8,128)(2,1)S(1)}, u32[]{:S(2)}, u32[]{:S(2)}) %collective-permute-start.19) | collective-permute-done | bytes 524320 | tf_op jit(solution)/shard_map/ppermute | solution.py:12
  345.5 12.2 %collective-permute-done.20 = bf16[32,1,64]{1,2,0:T(8,128)(2,1)S(1)} collective-permute-done((bf16[32,1,64]{1,2,0:T(8,128)(2,1)S(1)}, bf16[32,1,64]{1,2,0:T(8,128)(2,1)S(1)}, u32[]{:S(2)}, u32[]{:S(2)}) %collective-permute-start.20) | collective-permute-done | bytes 4128 | tf_op jit(solution)/shard_map/ppermute | solution.py:12
  361.9 12.2 %collective-permute-done.21 = bf16[32,2,64]{1,2,0:T(8,128)(2,1)S(1)} collective-permute-done((bf16[32,2,64]{1,2,0:T(8,128)(2,1)S(1)}, bf16[32,2,64]{1,2,0:T(8,128)(2,1)S(1)}, u32[]{:S(2)}, u32[]{:S(2)}) %collective-permute-start.21) | collective-permute-done | bytes 8224 | tf_op jit(solution)/shard_map/ppermute | solution.py:12
  395.7 12.2 %collective-permute-done.23 = bf16[32,8,64]{1,2,0:T(8,128)(2,1)S(1)} collective-permute-done((bf16[32,8,64]{1,2,0:T(8,128)(2,1)S(1)}, bf16[32,8,64]{1,2,0:T(8,128)(2,1)S(1)}, u32[]{:S(2)}, u32[]{:S(2)}) %collective-permute-start.23) | collective-permute-done | bytes 32800 | tf_op jit(solution)/shard_map/ppermute | solution.py:12
  413.2 12.2 %collective-permute-done.24 = bf16[32,16,64]{1,2,0:T(8,128)(2,1)S(1)} collective-permute-done((bf16[32,16,64]{1,2,0:T(8,128)(2,1)S(1)}, bf16[32,16,64]{1,2,0:T(8,128)(2,1)S(1)}, u32[]{:S(2)}, u32[]{:S(2)}) %collective-permute-start.24) | collective-permute-done | bytes 65568 | tf_op jit(solution)/shard_map/ppermute | solution.py:12
  429.6 12.2 %collective-permute-done.25 = bf16[32,32,64]{1,2,0:T(8,128)(2,1)S(1)} collective-permute-done((bf16[32,32,64]{1,2,0:T(8,128)(2,1)S(1)}, bf16[32,32,64]{1,2,0:T(8,128)(2,1)S(1)}, u32[]{:S(2)}, u32[]{:S(2)}) %collective-permute-start.25) | collective-permute-done | bytes 131104 | tf_op jit(solution)/shard_map/ppermute | solution.py:12
  447.1 12.2 %collective-permute-done.26 = bf16[32,64,64]{1,2,0:T(8,128)(2,1)S(1)} collective-permute-done((bf16[32,64,64]{1,2,0:T(8,128)(2,1)S(1)}, bf16[32,64,64]{1,2,0:T(8,128)(2,1)S(1)}, u32[]{:S(2)}, u32[]{:S(2)}) %collective-permute-start.26) | collective-permute-done | bytes 262176 | tf_op jit(solution)/shard_map/ppermute | solution.py:12
  463.3 12.2 %collective-permute-done.27 = bf16[32,128,64]{1,2,0:T(8,128)(2,1)S(1)} collective-permute-done((bf16[32,128,64]{1,2,0:T(8,128)(2,1)S(1)}, bf16[32,128,64]{1,2,0:T(8,128)(2,1)S(1)}, u32[]{:S(2)}, u32[]{:S(2)}) %collective-permute-start.27) | collective-permute-done | bytes 524320 | tf_op jit(solution)/shard_map/ppermute | solution.py:12
  480.8 12.6 %collective-permute-done.28 = bf16[32,128,64]{1,2,0:T(8,128)(2,1)S(1)} collective-permute-done((bf16[32,128,64]{1,2,0:T(8,128)(2,1)S(1)}, bf16[32,128,64]{1,2,0:T(8,128)(2,1)S(1)}, u32[]{:S(2)}, u32[]{:S(2)}) %collective-permute-start.28) | collective-permute-done | bytes 524320 | tf_op jit(solution)/shard_map/ppermute | solution.py:12
  497.3 13.1 %collective-permute-done.29 = bf16[32,128,64]{1,2,0:T(8,128)(2,1)S(1)} collective-permute-done((bf16[32,128,64]{1,2,0:T(8,128)(2,1)S(1)}, bf16[32,128,64]{1,2,0:T(8,128)(2,1)S(1)}, u32[]{:S(2)}, u32[]{:S(2)}) %collective-permute-start.29) | collective-permute-done | bytes 524320 | tf_op jit(solution)/shard_map/ppermute | solution.py:12
  (232 shorter events, 225.3 us)
Async XLA Ops:
  2.0 14.7 %collective-permute-start = (bf16[32,1,64]{1,2,0:T(8,128)(2,1)S(1)}, bf16[32,1,64]{1,2,0:T(8,128)(2,1)S(1)}, u32[]{:S(2)}, u32[]{:S(2)}) collective-permute-start(bf16[32,1,64]{1,2,0:T(8,128)(2,1)S(1)} %slice.757), channel_id=1, source_target_pairs={{0,1},{1,2},{2,3},{3,4},{4,5},{5,6},{6,7},{7,8},{8,9},{9,10},{10,1... | collective-permute-start | bytes 12296 | tf_op jit(solution)/shard_map/ppermute | solution.py:12
  19.0 14.9 %collective-permute-start.1 = (bf16[32,2,64]{1,2,0:T(8,128)(2,1)S(1)}, bf16[32,2,64]{1,2,0:T(8,128)(2,1)S(1)}, u32[]{:S(2)}, u32[]{:S(2)}) collective-permute-start(bf16[32,2,64]{1,2,0:T(8,128)(2,1)S(1)} %slice.1019), channel_id=1, source_target_pairs={{0,1},{1,2},{2,3},{3,4},{4,5},{5,6},{6,7},{7,8},{8,9},{9,10},{10,1... | collective-permute-start | bytes 24584 | tf_op jit(solution)/shard_map/ppermute | solution.py:12
  36.6 14.7 %collective-permute-start.2 = (bf16[32,4,64]{1,2,0:T(8,128)(2,1)S(1)}, bf16[32,4,64]{1,2,0:T(8,128)(2,1)S(1)}, u32[]{:S(2)}, u32[]{:S(2)}) collective-permute-start(bf16[32,4,64]{1,2,0:T(8,128)(2,1)S(1)} %slice.1030), channel_id=1, source_target_pairs={{0,1},{1,2},{2,3},{3,4},{4,5},{5,6},{6,7},{7,8},{8,9},{9,10},{10,1... | collective-permute-start | bytes 49160 | tf_op jit(solution)/shard_map/ppermute | solution.py:12
  53.0 14.7 %collective-permute-start.3 = (bf16[32,8,64]{1,2,0:T(8,128)(2,1)S(1)}, bf16[32,8,64]{1,2,0:T(8,128)(2,1)S(1)}, u32[]{:S(2)}, u32[]{:S(2)}) collective-permute-start(bf16[32,8,64]{1,2,0:T(8,128)(2,1)S(1)} %slice.1041), channel_id=1, source_target_pairs={{0,1},{1,2},{2,3},{3,4},{4,5},{5,6},{6,7},{7,8},{8,9},{9,10},{10,1... | collective-permute-start | bytes 98312 | tf_op jit(solution)/shard_map/ppermute | solution.py:12
  70.5 14.7 %collective-permute-start.4 = (bf16[32,16,64]{1,2,0:T(8,128)(2,1)S(1)}, bf16[32,16,64]{1,2,0:T(8,128)(2,1)S(1)}, u32[]{:S(2)}, u32[]{:S(2)}) collective-permute-start(bf16[32,16,64]{1,2,0:T(8,128)(2,1)S(1)} %slice.1052), channel_id=1, source_target_pairs={{0,1},{1,2},{2,3},{3,4},{4,5},{5,6},{6,7},{7,8},{8,9},{9,10},{10,1... | collective-permute-start | bytes 196616 | tf_op jit(solution)/shard_map/ppermute | solution.py:12
  86.9 14.7 %collective-permute-start.5 = (bf16[32,32,64]{1,2,0:T(8,128)(2,1)S(1)}, bf16[32,32,64]{1,2,0:T(8,128)(2,1)S(1)}, u32[]{:S(2)}, u32[]{:S(2)}) collective-permute-start(bf16[32,32,64]{1,2,0:T(8,128)(2,1)S(1)} %slice.1063), channel_id=1, source_target_pairs={{0,1},{1,2},{2,3},{3,4},{4,5},{5,6},{6,7},{7,8},{8,9},{9,10},{10,1... | collective-permute-start | bytes 393224 | tf_op jit(solution)/shard_map/ppermute | solution.py:12
  104.4 14.7 %collective-permute-start.6 = (bf16[32,64,64]{1,2,0:T(8,128)(2,1)S(1)}, bf16[32,64,64]{1,2,0:T(8,128)(2,1)S(1)}, u32[]{:S(2)}, u32[]{:S(2)}) collective-permute-start(bf16[32,64,64]{1,2,0:T(8,128)(2,1)S(1)} %get-tuple-element.34), channel_id=1, source_target_pairs={{0,1},{1,2},{2,3},{3,4},{4,5},{5,6},{6,7},{7,8},{8,9},{9,10},{10,1... | collective-permute-start | bytes 786440 | tf_op jit(solution)/shard_map/ppermute | solution.py:12
  120.5 14.7 %collective-permute-start.7 = (bf16[32,128,64]{1,2,0:T(8,128)(2,1)S(1)}, bf16[32,128,64]{1,2,0:T(8,128)(2,1)S(1)}, u32[]{:S(2)}, u32[]{:S(2)}) collective-permute-start(bf16[32,128,64]{1,2,0:T(8,128)(2,1)S(1)} %fusion.276), channel_id=1, source_target_pairs={{0,1},{1,2},{2,3},{3,4},{4,5},{5,6},{6,7},{7,8},{8,9},{9,10},{10,1... | collective-permute-start | bytes 1572872 | tf_op jit(solution)/shard_map/ppermute | solution.py:12
  137.8 15.3 %collective-permute-start.8 = (bf16[32,128,64]{1,2,0:T(8,128)(2,1)S(1)}, bf16[32,128,64]{1,2,0:T(8,128)(2,1)S(1)}, u32[]{:S(2)}, u32[]{:S(2)}) collective-permute-start(bf16[32,128,64]{1,2,0:T(8,128)(2,1)S(1)} %get-tuple-element.22), channel_id=1, source_target_pairs={{0,2},{1,3},{2,4},{3,5},{4,6},{5,7},{6,8},{7,9},{8,10},{9,11},{10,... | collective-permute-start | bytes 1572872 | tf_op jit(solution)/shard_map/ppermute | solution.py:12
  154.5 15.6 %collective-permute-start.9 = (bf16[32,128,64]{1,2,0:T(8,128)(2,1)S(1)}, bf16[32,128,64]{1,2,0:T(8,128)(2,1)S(1)}, u32[]{:S(2)}, u32[]{:S(2)}) collective-permute-start(bf16[32,128,64]{1,2,0:T(8,128)(2,1)S(1)} %fusion.277), channel_id=1, source_target_pairs={{0,4},{1,5},{2,6},{3,7},{4,8},{5,9},{6,10},{7,11},{8,12},{9,13},{1... | collective-permute-start | bytes 1572872 | tf_op jit(solution)/shard_map/ppermute | solution.py:12
  172.8 14.7 %collective-permute-start.10 = (bf16[32,1,64]{1,2,0:T(8,128)(2,1)S(1)}, bf16[32,1,64]{1,2,0:T(8,128)(2,1)S(1)}, u32[]{:S(2)}, u32[]{:S(2)}) collective-permute-start(bf16[32,1,64]{1,2,0:T(8,128)(2,1)S(1)} %slice.1112), channel_id=1, source_target_pairs={{0,1},{1,2},{2,3},{3,4},{4,5},{5,6},{6,7},{7,8},{8,9},{9,10},{10,1... | collective-permute-start | bytes 12296 | tf_op jit(solution)/shard_map/ppermute | solution.py:12
  189.2 14.7 %collective-permute-start.11 = (bf16[32,2,64]{1,2,0:T(8,128)(2,1)S(1)}, bf16[32,2,64]{1,2,0:T(8,128)(2,1)S(1)}, u32[]{:S(2)}, u32[]{:S(2)}) collective-permute-start(bf16[32,2,64]{1,2,0:T(8,128)(2,1)S(1)} %slice.1123), channel_id=1, source_target_pairs={{0,1},{1,2},{2,3},{3,4},{4,5},{5,6},{6,7},{7,8},{8,9},{9,10},{10,1... | collective-permute-start | bytes 24584 | tf_op jit(solution)/shard_map/ppermute | solution.py:12
  206.8 14.7 %collective-permute-start.12 = (bf16[32,4,64]{1,2,0:T(8,128)(2,1)S(1)}, bf16[32,4,64]{1,2,0:T(8,128)(2,1)S(1)}, u32[]{:S(2)}, u32[]{:S(2)}) collective-permute-start(bf16[32,4,64]{1,2,0:T(8,128)(2,1)S(1)} %slice.1134), channel_id=1, source_target_pairs={{0,1},{1,2},{2,3},{3,4},{4,5},{5,6},{6,7},{7,8},{8,9},{9,10},{10,1... | collective-permute-start | bytes 49160 | tf_op jit(solution)/shard_map/ppermute | solution.py:12
  223.1 14.7 %collective-permute-start.13 = (bf16[32,8,64]{1,2,0:T(8,128)(2,1)S(1)}, bf16[32,8,64]{1,2,0:T(8,128)(2,1)S(1)}, u32[]{:S(2)}, u32[]{:S(2)}) collective-permute-start(bf16[32,8,64]{1,2,0:T(8,128)(2,1)S(1)} %slice.1145), channel_id=1, source_target_pairs={{0,1},{1,2},{2,3},{3,4},{4,5},{5,6},{6,7},{7,8},{8,9},{9,10},{10,1... | collective-permute-start | bytes 98312 | tf_op jit(solution)/shard_map/ppermute | solution.py:12
  240.6 14.7 %collective-permute-start.14 = (bf16[32,16,64]{1,2,0:T(8,128)(2,1)S(1)}, bf16[32,16,64]{1,2,0:T(8,128)(2,1)S(1)}, u32[]{:S(2)}, u32[]{:S(2)}) collective-permute-start(bf16[32,16,64]{1,2,0:T(8,128)(2,1)S(1)} %slice.1156), channel_id=1, source_target_pairs={{0,1},{1,2},{2,3},{3,4},{4,5},{5,6},{6,7},{7,8},{8,9},{9,10},{10,1... | collective-permute-start | bytes 196616 | tf_op jit(solution)/shard_map/ppermute | solution.py:12
  256.9 14.7 %collective-permute-start.15 = (bf16[32,32,64]{1,2,0:T(8,128)(2,1)S(1)}, bf16[32,32,64]{1,2,0:T(8,128)(2,1)S(1)}, u32[]{:S(2)}, u32[]{:S(2)}) collective-permute-start(bf16[32,32,64]{1,2,0:T(8,128)(2,1)S(1)} %slice.1167), channel_id=1, source_target_pairs={{0,1},{1,2},{2,3},{3,4},{4,5},{5,6},{6,7},{7,8},{8,9},{9,10},{10,1... | collective-permute-start | bytes 393224 | tf_op jit(solution)/shard_map/ppermute | solution.py:12
  274.6 14.7 %collective-permute-start.16 = (bf16[32,64,64]{1,2,0:T(8,128)(2,1)S(1)}, bf16[32,64,64]{1,2,0:T(8,128)(2,1)S(1)}, u32[]{:S(2)}, u32[]{:S(2)}) collective-permute-start(bf16[32,64,64]{1,2,0:T(8,128)(2,1)S(1)} %get-tuple-element.32), channel_id=1, source_target_pairs={{0,1},{1,2},{2,3},{3,4},{4,5},{5,6},{6,7},{7,8},{8,9},{9,10},{10,1... | collective-permute-start | bytes 786440 | tf_op jit(solution)/shard_map/ppermute | solution.py:12
  290.7 14.7 %collective-permute-start.17 = (bf16[32,128,64]{1,2,0:T(8,128)(2,1)S(1)}, bf16[32,128,64]{1,2,0:T(8,128)(2,1)S(1)}, u32[]{:S(2)}, u32[]{:S(2)}) collective-permute-start(bf16[32,128,64]{1,2,0:T(8,128)(2,1)S(1)} %fusion.281), channel_id=1, source_target_pairs={{0,1},{1,2},{2,3},{3,4},{4,5},{5,6},{6,7},{7,8},{8,9},{9,10},{10,1... | collective-permute-start | bytes 1572872 | tf_op jit(solution)/shard_map/ppermute | solution.py:12
  308.0 15.3 %collective-permute-start.18 = (bf16[32,128,64]{1,2,0:T(8,128)(2,1)S(1)}, bf16[32,128,64]{1,2,0:T(8,128)(2,1)S(1)}, u32[]{:S(2)}, u32[]{:S(2)}) collective-permute-start(bf16[32,128,64]{1,2,0:T(8,128)(2,1)S(1)} %get-tuple-element.12), channel_id=1, source_target_pairs={{0,2},{1,3},{2,4},{3,5},{4,6},{5,7},{6,8},{7,9},{8,10},{9,11},{10,... | collective-permute-start | bytes 1572872 | tf_op jit(solution)/shard_map/ppermute | solution.py:12
  324.7 15.6 %collective-permute-start.19 = (bf16[32,128,64]{1,2,0:T(8,128)(2,1)S(1)}, bf16[32,128,64]{1,2,0:T(8,128)(2,1)S(1)}, u32[]{:S(2)}, u32[]{:S(2)}) collective-permute-start(bf16[32,128,64]{1,2,0:T(8,128)(2,1)S(1)} %fusion.282), channel_id=1, source_target_pairs={{0,4},{1,5},{2,6},{3,7},{4,8},{5,9},{6,10},{7,11},{8,12},{9,13},{1... | collective-permute-start | bytes 1572872 | tf_op jit(solution)/shard_map/ppermute | solution.py:12
  343.0 14.7 %collective-permute-start.20 = (bf16[32,1,64]{1,2,0:T(8,128)(2,1)S(1)}, bf16[32,1,64]{1,2,0:T(8,128)(2,1)S(1)}, u32[]{:S(2)}, u32[]{:S(2)}) collective-permute-start(bf16[32,1,64]{1,2,0:T(8,128)(2,1)S(1)} %slice.1216), channel_id=1, source_target_pairs={{0,1},{1,2},{2,3},{3,4},{4,5},{5,6},{6,7},{7,8},{8,9},{9,10},{10,1... | collective-permute-start | bytes 12296 | tf_op jit(solution)/shard_map/ppermute | solution.py:12
  410.7 14.7 %collective-permute-start.24 = (bf16[32,16,64]{1,2,0:T(8,128)(2,1)S(1)}, bf16[32,16,64]{1,2,0:T(8,128)(2,1)S(1)}, u32[]{:S(2)}, u32[]{:S(2)}) collective-permute-start(bf16[32,16,64]{1,2,0:T(8,128)(2,1)S(1)} %slice.1260), channel_id=1, source_target_pairs={{0,1},{1,2},{2,3},{3,4},{4,5},{5,6},{6,7},{7,8},{8,9},{9,10},{10,1... | collective-permute-start | bytes 196616 | tf_op jit(solution)/shard_map/ppermute | solution.py:12
  478.1 15.3 %collective-permute-start.28 = (bf16[32,128,64]{1,2,0:T(8,128)(2,1)S(1)}, bf16[32,128,64]{1,2,0:T(8,128)(2,1)S(1)}, u32[]{:S(2)}, u32[]{:S(2)}) collective-permute-start(bf16[32,128,64]{1,2,0:T(8,128)(2,1)S(1)} %get-tuple-element.2), channel_id=1, source_target_pairs={{0,2},{1,3},{2,4},{3,5},{4,6},{5,7},{6,8},{7,9},{8,10},{9,11},{10,... | collective-permute-start | bytes 1572872 | tf_op jit(solution)/shard_map/ppermute | solution.py:12
  494.8 15.6 %collective-permute-start.29 = (bf16[32,128,64]{1,2,0:T(8,128)(2,1)S(1)}, bf16[32,128,64]{1,2,0:T(8,128)(2,1)S(1)}, u32[]{:S(2)}, u32[]{:S(2)}) collective-permute-start(bf16[32,128,64]{1,2,0:T(8,128)(2,1)S(1)} %fusion.287), channel_id=1, source_target_pairs={{0,4},{1,5},{2,6},{3,7},{4,8},{5,9},{6,10},{7,11},{8,12},{9,13},{1... | collective-permute-start | bytes 1572872 | tf_op jit(solution)/shard_map/ppermute | solution.py:12
  (33 other events, 245.5 us)
where the time goes:
time: 534 us; the launch traced here: 526 us
  waiting for transfers between devices  369 us (69%)
  starting transfers between devices  59 us (11%)
  matrix products  55.4 us (10%)
  local copies, waits for them, and re-layouts  20.4 us (4%)
  other arithmetic  19.2 us (4%)
    ppermute x30, waiting for transfers between devices, move_right(): lax.ppermute(block, SEQ_AXES, perm=[(source, source + hops) for source in...  369 us
    ppermute x30, starting transfers between devices, move_right(): lax.ppermute(block, SEQ_AXES, perm=[(source, source + hops) for source in...  59 us
    dot_general x30, matrix products, gated_layer(): jnp.einsum('bsc,cd->bsd', activated, w_out, preferred_element_type=jnp.fl...  21.1 us
    dot_general x30, matrix products, gated_layer(): jnp.einsum('bsc,cd->bsd', current, w_cur, preferred_element_type=jnp.floa...  17.4 us
    dot_general x30, matrix products, gated_layer(): jnp.einsum('bsc,cd->bsd', delayed, w_del, preferred_element_type=jnp.floa...  17 us
    unnamed x54, local copies, waits for them, and re-layouts  14.7 us
    add x2, other arithmetic, gated_layer(): return (residual + mixed[..., :chans], skip_acc + mixed[..., chans:])  12.4 us
  transfers between devices with their start and end apart: 30, of which 30 were waited for; matrix products, arithmetic and copies ran while one was open for 3% of the time, Pallas kernels for 0%

commit v1 on v0

v1 whole, which is shorter than its diff:
```python
import jax
import jax.numpy as jnp
from jax import lax
from jax.experimental import pallas as pl
from jax.experimental.pallas import tpu as pltpu
from jax.sharding import PartitionSpec as P

F32, BF = jnp.float32, jnp.bfloat16
SEQ_AXES = ("seq_hi", "seq")
NT = 8
HALO = 24
LAG1, LAG2 = 5, 4
CHANS, TILE, CYCLE = 64, 128, 10


def run_layers(reps, hs, ss, acts, us, hist, w1t, wrt, wst, lane):
    items = [(c, st, j) for c in range(CYCLE) for st in range(len(reps)) for j in range(0, NT, 2)]
    carry, gates, mixed, skips = {}, {}, {}, {}

    def front(t):
        c, st, j = items[t]
        d = 2**c
        nh = max(1, d // TILE)
        layer = reps[st] * CYCLE + c
        h, ub = hs[st], us[st]
        if j == 0:
            for i in range(4 - nh, 4):
                ub[i] = hist[layer, i]
            if d < TILE:
                carry[st] = pltpu.roll(ub[3], d, 1)
        u = [h[j].astype(BF), h[j + 1].astype(BF)]
        if d >= TILE:
            ub[4 + j], ub[5 + j] = u[0], u[1]
            q = d // TILE
            p = [ub[4 + j - q], ub[5 + j - q] if q > 1 else u[0]]
        else:
            r0, r1 = pltpu.roll(u[0], d, 1), pltpu.roll(u[1], d, 1)
            p = [jnp.where(lane < d, carry[st], r0), jnp.where(lane < d, r0, r1)]
            carry[st] = r1
        for i in range(2):
            k = j + i - (NT - 4)
            if k >= 4 - nh:
                hist[layer, k] = u[i]
        up = jnp.concatenate([jnp.concatenate(u, 1), jnp.concatenate(p, 1)], 0)
        gates[t] = jnp.dot(w1t[layer], up, preferred_element_type=F32)

    def middle(t):
        c, st, j = items[t]
        layer = reps[st] * CYCLE + c
        g = gates.pop(t)
        sig = jnp.tanh(g[CHANS:] * 0.5) * 0.5 + 0.5
        a = (jnp.tanh(g[:CHANS]) * sig).astype(BF)
        row = (c % 4) * CHANS
        cols = slice(j * TILE, (j + 2) * TILE)
        if c not in (3, 7, 9):
            acts[st][row : row + CHANS, cols] = a
        mixed[t] = jnp.dot(wrt[layer], a, preferred_element_type=F32)
        if c in (3, 7, 9):
            stack = jnp.concatenate([acts[st][:row, cols], a], 0)
            skips[t] = jnp.dot(wst[reps[st] * 3 + c // 4][:, : row + CHANS], stack, preferred_element_type=F32)

    def back(t):
        c, st, j = items[t]
        res = mixed.pop(t)
        h = hs[st]
        h[j] += res[:, :TILE]
        h[j + 1] += res[:, TILE:]
        if t in skips:
            res = skips.pop(t)
            ss[st][j] += res[:, :TILE]
            ss[st][j + 1] += res[:, TILE:]

    n = len(items)
    for t in range(n + LAG1 + LAG2):
        if t >= LAG1 + LAG2:
            back(t - LAG1 - LAG2)
        if t < n:
            front(t)
        if 0 <= t - LAG1 < n:
            middle(t - LAG1)


def kernel(x, w1t, wrt, wst, hout, sout, xbuf, hA, hB, hC, sA, sB, sC, aA, aB, aC, uA, uB, uC, hist, hstage, sstage,
           in_send, in_recv, halo_send, out_send, out_recv):
    hi, k = lax.axis_index("seq_hi"), lax.axis_index("seq")
    z, row = hi // 4, hi % 4
    me = row * 8 + k

    def device(zz, m):
        return {"seq_hi": zz * 4 + m // 8, "seq": m % 8}

    def own_copy(s):
        return pltpu.make_async_remote_copy(
            src_ref=x.at[s], dst_ref=xbuf.at[HALO + me], send_sem=in_send.at[s], recv_sem=in_recv.at[HALO + me],
            device_id=device(z, s), device_id_type=pl.DeviceIdType.MESH)

    def halo_copy(s):
        return pltpu.make_async_remote_copy(
            src_ref=x.at[s], dst_ref=xbuf.at[me - 8], send_sem=halo_send.at[s], recv_sem=in_recv.at[me - 8],
            device_id=device(z + 1, s), device_id_type=pl.DeviceIdType.MESH)

    def out_copy(i, src, dst, m):
        return pltpu.make_async_remote_copy(
            src_ref=src.at[m], dst_ref=dst.at[me], send_sem=out_send.at[i, m], recv_sem=out_recv.at[i, me],
            device_id=device(z, m), device_id_type=pl.DeviceIdType.MESH)

    sends_halo = jnp.logical_and(z < 3, row >= 1)

    @pl.when(sends_halo)
    def _():
        def start(o, c):
            halo_copy(lax.rem(me + o, 32)).start()
            return c
        lax.fori_loop(0, 32, start, 0)

    def start_own(o, c):
        own_copy(lax.rem(me + o, 32)).start()
        return c

    lax.fori_loop(1, 32, start_own, 0)

    lane = lax.broadcasted_iota(jnp.int32, (CHANS, TILE), 1)
    hist[...] = jnp.zeros_like(hist)
    xbuf[HALO + me] = x[me]

    @pl.when(z == 0)
    def _():
        xbuf[0:HALO] = jnp.zeros((HALO, CHANS, TILE), BF)

    def wait_tile(t):
        pltpu.make_async_copy(xbuf.at[t], xbuf.at[t], in_recv.at[t]).wait()

    @pl.when(z > 0)
    def _():
        def w(t, c):
            wait_tile(t)
            return c
        lax.fori_loop(0, HALO, w, 0)

    def macro(s):
        @pl.when(s >= 3)
        def _():
            hC[...] = hB[...]
            sC[...] = sB[...]

        @pl.when(s >= 2)
        def _():
            hB[...] = hA[...]
            sB[...] = sA[...]

        @pl.when(s == 0)
        def _():
            hA[...] = xbuf[0:8].astype(F32)
            hB[...] = xbuf[8:16].astype(F32)
            hC[...] = xbuf[16:24].astype(F32)
            for ref in (sA, sB, sC):
                ref[...] = jnp.zeros_like(ref)

        @pl.when(jnp.logical_and(s >= 1, s <= 4))
        def _():
            base = (s + 2) * NT

            def w(i, c):
                @pl.when(base + i != HALO + me)
                def _():
                    wait_tile(base + i)
                return c

            lax.fori_loop(0, NT, w, 0)
            hA[...] = xbuf[pl.ds(base, NT)].astype(F32)
            sA[...] = jnp.zeros_like(sA)

        reps = [0, jnp.minimum(s, 1), jnp.minimum(s, 2)]
        run_layers(reps, [hA, hB, hC], [sA, sB, sC], [aA, aB, aC], [uA, uB, uC], hist, w1t, wrt, wst, lane)

        @pl.when(s >= 3)
        def _():
            base = (s - 3) * NT
            hstage[pl.ds(base, NT)] = hC[...]
            sstage[pl.ds(base, NT)] = sC[...]

            def send(o, c):
                m = base + lax.rem(o + k, NT)

                @pl.when(m != me)
                def _():
                    out_copy(0, hstage, hout, m).start()
                    out_copy(1, sstage, sout, m).start()
                return c

            lax.fori_loop(0, NT, send, 0)

    lax.fori_loop(0, 7, lambda s, c: (macro(s), c)[1], 0)

    hout[me] = hstage[me]
    sout[me] = sstage[me]

    @pl.when(sends_halo)
    def _():
        def w(s, c):
            halo_copy(s).wait_send()
            return c
        lax.fori_loop(0, 32, w, 0)

    def drain(o, c):
        m = lax.rem(me + o, 32)
        own_copy(m).wait_send()
        out_copy(0, hstage, hout, m).wait_send()
        out_copy(1, sstage, sout, m).wait_send()
        pltpu.make_async_copy(hout.at[m], hout.at[m], out_recv.at[0, m]).wait()
        pltpu.make_async_copy(sout.at[m], sout.at[m], out_recv.at[1, m]).wait()
        return c

    lax.fori_loop(1, 32, drain, 0)


def solution(mesh):
    seq_spec = P("batch", SEQ_AXES, None)

    def local_stack(x_loc, w_f0, w_f1, w_g0, w_g1, w_res, w_skip):
        x_t = jnp.swapaxes(x_loc, 1, 2)
        flat = lambda w: jnp.swapaxes(w.reshape(30, CHANS, CHANS), 1, 2)
        w1t = jnp.concatenate([jnp.concatenate([flat(w_f1), flat(w_f0)], 2), jnp.concatenate([flat(w_g1), flat(w_g0)], 2)], 1)
        wrt = flat(w_res)
        ws = jnp.pad(jnp.swapaxes(w_skip, 2, 3), ((0, 0), (0, 2), (0, 0), (0, 0)))
        wst = ws.reshape(3, 3, 4, CHANS, CHANS).transpose(0, 1, 3, 2, 4).reshape(9, CHANS, 4 * CHANS)
        V, D = pltpu.VMEM, pltpu.SemaphoreType.DMA
        hid = (NT, CHANS, TILE)
        out = jax.ShapeDtypeStruct((32, CHANS, TILE), F32)
        h, skip = pl.pallas_call(
            kernel,
            out_shape=[out, out],
            in_specs=[pl.BlockSpec(memory_space=V)] * 4,
            out_specs=[pl.BlockSpec(memory_space=V)] * 2,
            scratch_shapes=[V((56, CHANS, TILE), BF)] + [V(hid, F32)] * 6 + [V((4 * CHANS, NT * TILE), BF)] * 3
            + [V((NT + 4, CHANS, TILE), BF)] * 3 + [V((30, 4, CHANS, TILE), BF)] + [V((32, CHANS, TILE), F32)] * 2
            + [D((32,)), D((56,)), D((32,)), D((2, 32)), D((2, 32))],
            compiler_params=pltpu.CompilerParams(vmem_limit_bytes=60 * 2**20, has_side_effects=True),
        )(x_t, w1t, wrt, wst)
        return jnp.swapaxes(h, 1, 2), jnp.swapaxes(skip, 1, 2)

    return jax.shard_map(local_stack, mesh=mesh, in_specs=(seq_spec, P(), P(), P(), P(), P(), P()), out_specs=(seq_spec, seq_spec), check_vma=False)
```

time: 534 us -> 101 us (0.19)
  the two profiles are of different devices: /device:TPU:96 before, /device:TPU:121 now
where the time goes in v1:
time: 101 us; the launch traced here: 100 us
  Pallas kernels  88.8 us (88%)
  local copies, waits for them, and re-layouts  9.3 us (9%)
  other arithmetic  1.49 us (1%)
    pallas_call x1, Pallas kernels, local_stack(): pl.pallas_call(kernel, out_shape=[out, out], in_specs=[pl.BlockSpec(memor...  88.8 us
    unnamed x19, local copies, waits for them, and re-layouts  7.05 us
    reshape x2, local copies, waits for them, and re-layouts, local_stack(): ws.reshape(3, 3, 4, CHANS, CHANS).transpose(0, 1, 3, 2, 4)  2.13 us

profile of v1, /device:TPU:121, one launch (start us, length us, event | category | flops | bytes accessed | tf_op | source)
XLA Modules:
  0.0 100.3 jit_solution(10526052269464360474)
XLA Ops:
  0.6 0.0 copy-start.2
  0.6 0.0 copy-start.1
  0.7 1.4 %copy.10 = bf16[3,10,64,64]{2,3,1,0:T(8,128)(2,1)S(1)} copy(bf16[3,10,64,64]{3,2,1,0:T(8,128)(2,1)} %param.8) | data formatting | bytes 491520 | tf_op args[1]
  2.0 0.0 copy-start.3
  2.0 0.0 copy-done.1
  2.0 0.3 copy.9
  2.3 0.0 copy-done.2
  2.3 0.3 copy.12
  2.6 0.5 copy-done.3
  3.1 0.3 copy.11
  3.3 0.0 copy-start.4
  3.3 1.5 %maximum_maximum_fusion.w1t = bf16[30,128,128]{2,1,0:T(8,128)(2,1)} fusion(bf16[30,64,64]{2,1,0:T(8,128)(2,1)S(1)} %bitcast.26, bf16[30,64,64]{2,1,0:T(8,128)(2,1)S(1)} %bitcast.27, bf16[30,64,64]{2,1,0:T(8,128)(2,1)S(1)} %bitcast.24, bf16[30,64,64]{2,1,0:T(8,128)(2,1)S(1)} %bitcast.25), kind=kLoop, calls=%fused_computation | loop fusion | flops 3932160 | bytes 1966080 | tf_op jit(solution)/shard_map/concatenate | solution.py:223
  4.8 0.0 copy-done.4
  4.8 0.0 copy-start.5
  4.8 1.0 copy.13
  5.8 0.0 copy-done.5
  5.9 0.1 pad.4
  6.0 1.0 %copy.14 = bf16[3,3,4,64,64]{4,2,3,1,0:T(4,128)(2,1)S(1)} copy(bf16[3,3,4,64,64]{3,4,2,1,0:T(8,128)(2,1)S(1)} %bitcast.21) | data formatting | bytes 589824 | tf_op jit(solution)/shard_map/reshape | solution.py:226
  7.0 1.1 %reshape.31.wst = bf16[9,64,256]{2,1,0:T(8,128)(2,1)} reshape(bf16[3,3,64,4,64]{4,3,2,1,0:T(4,128)(2,1)S(1)} %bitcast.22) | data formatting | bytes 589824 | tf_op jit(solution)/shard_map/reshape | solution.py:226
  8.1 88.8 %shard_map.86 = (f32[32,64,128]{2,1,0:T(8,128)}, f32[32,64,128]{2,1,0:T(8,128)}) custom-call(bf16[32,64,128]{2,1,0:T(8,128)(2,1)} %bitcast.30, bf16[30,128,128]{2,1,0:T(8,128)(2,1)} %maximum_maximum_fusion.w1t, bf16[30,64,64]{2,1,0:T(8,128)(2,1)} %bitcast.23, bf16[9,64,256]{2,1,0:T(8,128)(2,1)} %reshape.31.wst), custom_call_target="tpu_custom_call" | custom-call | tf_op jit(solution)/shard_map/pallas_call | solution.py:230
  96.9 0.0 copy-start
  96.9 2.4 %copy.17 = f32[32,128,64]{1,2,0:T(8,128)} copy(f32[32,128,64]{1,2,0:T(8,128)} %bitcast.29) | data formatting | bytes 2097152
  99.3 0.0 copy-done
  99.3 1.0 copy.18
Async XLA Ops:
  0.6 1.7 %copy-start.2 = (bf16[3,10,64,64]{3,2,1,0:T(8,128)(2,1)S(1)}, bf16[3,10,64,64]{3,2,1,0:T(8,128)(2,1)}, u32[]{:S(2)}) copy-start(bf16[3,10,64,64]{3,2,1,0:T(8,128)(2,1)} %param.10) | copy-start | bytes 737284
  0.6 1.4 %copy-start.1 = (bf16[3,10,64,64]{3,2,1,0:T(8,128)(2,1)S(1)}, bf16[3,10,64,64]{3,2,1,0:T(8,128)(2,1)}, u32[]{:S(2)}) copy-start(bf16[3,10,64,64]{3,2,1,0:T(8,128)(2,1)} %param.9) | copy-start | bytes 737284
  2.0 1.0 %copy-start.3 = (bf16[3,10,64,64]{3,2,1,0:T(8,128)(2,1)S(1)}, bf16[3,10,64,64]{3,2,1,0:T(8,128)(2,1)}, u32[]{:S(2)}) copy-start(bf16[3,10,64,64]{3,2,1,0:T(8,128)(2,1)} %param.11) | copy-start | bytes 737284
  3.3 1.5 %copy-start.4 = (bf16[3,10,64,64]{3,2,1,0:T(8,128)(2,1)S(1)}, bf16[3,10,64,64]{3,2,1,0:T(8,128)(2,1)}, u32[]{:S(2)}) copy-start(bf16[3,10,64,64]{3,2,1,0:T(8,128)(2,1)} %param.12) | copy-start | bytes 737284
  4.8 1.0 %copy-start.5 = (bf16[3,10,64,64]{3,2,1,0:T(8,128)(2,1)S(1)}, bf16[3,10,64,64]{3,2,1,0:T(8,128)(2,1)}, u32[]{:S(2)}) copy-start(bf16[3,10,64,64]{3,2,1,0:T(8,128)(2,1)} %param.13) | copy-start | bytes 737284
  96.9 2.4 %copy-start = (f32[32,64,128]{2,1,0:T(8,128)S(1)}, f32[32,64,128]{2,1,0:T(8,128)}, u32[]{:S(2)}) copy-start(f32[32,64,128]{2,1,0:T(8,128)} %get-tuple-element.5) | copy-start | bytes 3145732

commit v2 on v1

v2 whole, which is shorter than its diff:
```python
import jax
import jax.numpy as jnp
from jax import lax
from jax.experimental import pallas as pl
from jax.experimental.pallas import tpu as pltpu
from jax.sharding import PartitionSpec as P

F32, BF = jnp.float32, jnp.bfloat16
SEQ_AXES = ("seq_hi", "seq")
MESH = pl.DeviceIdType.MESH
NT = 8
HALO = 24
LAG1, LAG2 = 5, 4
ZERO = 30
CHANS, TILE, CYCLE = 64, 128, 10


def run_layers(reps, resets, hs, ss, acts, us, hist, w1t, wrt, wst, lane):
    items = [(c, st, j) for c in range(CYCLE) for st in range(len(reps)) for j in range(0, NT, 2)]
    carry, gates, mixed, skips = {}, {}, {}, {}

    def front(t):
        c, st, j = items[t]
        d = 2**c
        nh = max(1, d // TILE)
        layer = reps[st] * CYCLE + c
        h, ub = hs[st], us[st]
        if j == 0:
            for i in range(4 - nh, 4):
                ub[i] = hist[jnp.where(resets[st], ZERO, layer), i]
            if d < TILE:
                carry[st] = pltpu.roll(ub[3], d, 1)
        u = [h[j].astype(BF), h[j + 1].astype(BF)]
        if d >= TILE:
            ub[4 + j], ub[5 + j] = u[0], u[1]
            q = d // TILE
            p = [ub[4 + j - q], ub[5 + j - q] if q > 1 else u[0]]
        else:
            r0, r1 = pltpu.roll(u[0], d, 1), pltpu.roll(u[1], d, 1)
            p = [jnp.where(lane < d, carry[st], r0), jnp.where(lane < d, r0, r1)]
            carry[st] = r1
        for i in range(2):
            k = j + i - (NT - 4)
            if k >= 4 - nh:
                hist[layer, k] = u[i]
        up = jnp.concatenate([jnp.concatenate(u, 1), jnp.concatenate(p, 1)], 0)
        gates[t] = jnp.dot(w1t[layer], up, preferred_element_type=F32)

    def middle(t):
        c, st, j = items[t]
        layer = reps[st] * CYCLE + c
        g = gates.pop(t)
        sig = jnp.tanh(g[CHANS:] * 0.5) * 0.5 + 0.5
        a = (jnp.tanh(g[:CHANS]) * sig).astype(BF)
        row = (c % 4) * CHANS
        cols = slice(j * TILE, (j + 2) * TILE)
        if c not in (3, 7, 9):
            acts[st][row : row + CHANS, cols] = a
        mixed[t] = jnp.dot(wrt[layer], a, preferred_element_type=F32)
        if c in (3, 7, 9):
            stack = jnp.concatenate([acts[st][:row, cols], a], 0)
            ws = jnp.concatenate([wst[layer - c % 4 + i] for i in range(c % 4 + 1)], 1)
            skips[t] = jnp.dot(ws, stack, preferred_element_type=F32)

    def back(t):
        c, st, j = items[t]
        res = mixed.pop(t)
        h = hs[st]
        h[j] += res[:, :TILE]
        h[j + 1] += res[:, TILE:]
        if t in skips:
            res = skips.pop(t)
            ss[st][j] += res[:, :TILE]
            ss[st][j + 1] += res[:, TILE:]

    n = len(items)
    for t in range(n + LAG1 + LAG2):
        if t >= LAG1 + LAG2:
            back(t - LAG1 - LAG2)
        if t < n:
            front(t)
        if 0 <= t - LAG1 < n:
            middle(t - LAG1)


def shift_of(s):
    return lax.rem((s % 8) // 2 + s % 2, 4)


def kernel(x_hbm, wf0, wf1, wg0, wg1, wres, wskip, hout, sout, x, w0, w1, w2, w3, w4, w5, w1t, wrt, wst, xbuf,
           hA, hB, hC, sA, sB, sC, aA, aB, aC, uA, uB, uC, hist, hstage, sstage,
           load_sem, in_send, in_recv, halo_send, out_send, out_recv):
    loads = [pltpu.make_async_copy(a, b, load_sem.at[i])
             for i, (a, b) in enumerate(zip((x_hbm, wf0, wf1, wg0, wg1, wres, wskip), (x, w0, w1, w2, w3, w4, w5)))]
    for load in loads:
        load.start()
    hi, k = lax.axis_index("seq_hi"), lax.axis_index("seq")
    z, row = hi // 4, hi % 4
    me = row * 8 + k
    first = 4 * z + shift_of(me)

    def device(h, m):
        return {"seq_hi": h, "seq": m}

    def place(s):
        e = lax.rem(hi - shift_of(s) + 16, 16)
        return e // 4, e % 4

    def own_copy(s):
        q, c = place(s)
        slot = (3 + c) * NT + k
        go = jnp.logical_or(q != z, s != me)
        return go, pltpu.make_async_remote_copy(
            src_ref=x.at[s], dst_ref=xbuf.at[slot], send_sem=in_send.at[s], recv_sem=in_recv.at[slot],
            device_id=device(q * 4 + s // 8, s % 8), device_id_type=MESH)

    def halo_copy(s):
        q, c = place(s)
        nxt = lax.rem(q + 1, 4)
        slot = lax.rem(c + 3, 4) * NT + k
        go = jnp.logical_and(c >= 1, jnp.logical_or(q != 3, hi < shift_of(s)))
        go = jnp.logical_and(go, jnp.logical_or(nxt != z, s != me))
        return go, pltpu.make_async_remote_copy(
            src_ref=x.at[s], dst_ref=xbuf.at[slot], send_sem=halo_send.at[s], recv_sem=in_recv.at[slot],
            device_id=device(nxt * 4 + s // 8, s % 8), device_id_type=MESH)

    def source(slot):
        g = first - 3 + slot // NT
        src = lax.rem(g + 16, 16)
        return g, src, jnp.logical_and(g >= 0, jnp.logical_or(src != hi, slot % NT != k))

    def out_copy(i, src, dst, t):
        g = lax.rem(first + t // NT, 16)
        return pltpu.make_async_remote_copy(
            src_ref=src.at[t], dst_ref=dst.at[me], send_sem=out_send.at[i, t], recv_sem=out_recv.at[i, me],
            device_id=device(g, t % NT), device_id_type=MESH)

    def out_goes(t):
        return jnp.logical_or(lax.rem(first + t // NT, 16) != hi, t % NT != k)

    def order(o):
        return lax.rem(me + 5 * o, 32)

    barrier = pltpu.get_barrier_semaphore()

    def greet(slot, c):
        g, src, remote = source(slot)

        @pl.when(remote)
        def _():
            pl.semaphore_signal(barrier, inc=1, device_id=device(src, slot % NT), device_id_type=MESH)
        return c

    lax.fori_loop(0, 56, greet, 0)
    peers = lax.fori_loop(0, 32, lambda s, n: n + own_copy(s)[0].astype(jnp.int32) + halo_copy(s)[0].astype(jnp.int32), jnp.int32(0))
    loads[0].wait()
    pl.semaphore_wait(barrier, peers)

    def start_halo(o, c):
        go, copy = halo_copy(order(o))
        pl.when(go)(copy.start)
        return c

    def start_own(o, c):
        go, copy = own_copy(order(o))
        pl.when(go)(copy.start)
        return c

    lax.fori_loop(0, 32, start_halo, 0)
    lax.fori_loop(0, 32, start_own, 0)

    for load in loads[1:]:
        load.wait()

    def prepare(c, carry):
        for r in range(3):
            layer = r * CYCLE + c
            top = jnp.concatenate([w1[r, c], w3[r, c]], 1)
            low = jnp.concatenate([w0[r, c], w2[r, c]], 1)
            w1t[layer] = jnp.concatenate([top, low], 0).astype(F32).T.astype(BF)
            last = jnp.concatenate([w4[r, c], w5[r, c]], 1).astype(F32).T.astype(BF)
            wrt[layer] = last[:CHANS]
            wst[layer] = last[CHANS:]
        return carry

    lax.fori_loop(0, CYCLE, prepare, 0)

    lane = lax.broadcasted_iota(jnp.int32, (CHANS, TILE), 1)
    hist[...] = jnp.zeros_like(hist)
    xbuf[(3 + row - shift_of(me)) * NT + k] = x[me]
    for kk in range(3):
        @pl.when(first - 3 + kk < 0)
        def _():
            xbuf[kk * NT : (kk + 1) * NT] = jnp.zeros((NT, CHANS, TILE), BF)

    def wait_slot(slot, c):
        @pl.when(source(slot)[2])
        def _():
            pltpu.make_async_copy(xbuf.at[slot], xbuf.at[slot], in_recv.at[slot]).wait()
        return c

    lax.fori_loop(0, 3 * NT, wait_slot, 0)

    def macro(s):
        @pl.when(s >= 3)
        def _():
            hC[...] = hB[...]
            sC[...] = sB[...]

        @pl.when(s >= 2)
        def _():
            hB[...] = hA[...]
            sB[...] = sA[...]

        @pl.when(s == 0)
        def _():
            hA[...] = xbuf[0:8].astype(F32)
            hB[...] = xbuf[8:16].astype(F32)
            hC[...] = xbuf[16:24].astype(F32)
            for ref in (sA, sB, sC):
                ref[...] = jnp.zeros_like(ref)

        @pl.when(jnp.logical_and(s >= 1, s <= 4))
        def _():
            base = (s + 2) * NT
            lax.fori_loop(base, base + NT, wait_slot, 0)
            hA[...] = xbuf[pl.ds(base, NT)].astype(F32)
            sA[...] = jnp.zeros_like(sA)

        reps = [0, jnp.minimum(s, 1), jnp.minimum(s, 2)]
        resets = [first - 3 + s + i == 16 for i in (2, 1, 0)]
        run_layers(reps, resets, [hA, hB, hC], [sA, sB, sC], [aA, aB, aC], [uA, uB, uC], hist, w1t, wrt, wst, lane)

        @pl.when(s >= 3)
        def _():
            base = (s - 3) * NT
            hstage[pl.ds(base, NT)] = hC[...]
            sstage[pl.ds(base, NT)] = sC[...]

            def send(o, c):
                t = base + lax.rem(3 * o + k, NT)

                @pl.when(out_goes(t))
                def _():
                    out_copy(0, hstage, hout, t).start()
                    out_copy(1, sstage, sout, t).start()
                return c

            lax.fori_loop(0, NT, send, 0)

    lax.fori_loop(0, 7, lambda s, c: (macro(s), c)[1], 0)

    keeps = row >= shift_of(me)

    @pl.when(keeps)
    def _():
        t = (row - shift_of(me)) * NT + k
        hout[me] = hstage[t]
        sout[me] = sstage[t]

    def drain(s, c):
        for go, copy in (own_copy(s), halo_copy(s)):
            pl.when(go)(copy.wait_send)

        @pl.when(out_goes(s))
        def _():
            out_copy(0, hstage, hout, s).wait_send()
            out_copy(1, sstage, sout, s).wait_send()

        @pl.when(own_copy(s)[0])
        def _():
            pltpu.make_async_copy(hout.at[s], hout.at[s], out_recv.at[0, s]).wait()
            pltpu.make_async_copy(sout.at[s], sout.at[s], out_recv.at[1, s]).wait()
        return c

    lax.fori_loop(0, 32, drain, 0)


def solution(mesh):
    seq_spec = P("batch", SEQ_AXES, None)

    def local_stack(x_loc, *weights):
        x_t = jnp.swapaxes(x_loc, 1, 2)
        V, D = pltpu.VMEM, pltpu.SemaphoreType.DMA
        hid = (NT, CHANS, TILE)
        out = jax.ShapeDtypeStruct((32, CHANS, TILE), F32)
        h, skip = pl.pallas_call(
            kernel,
            out_shape=[out, out],
            in_specs=[pl.BlockSpec(memory_space=pl.ANY)] * 7,
            out_specs=[pl.BlockSpec(memory_space=V)] * 2,
            scratch_shapes=[V((32, CHANS, TILE), BF)] + [V((3, CYCLE, CHANS, CHANS), BF)] * 6
            + [V((30, 2 * CHANS, 2 * CHANS), BF)] + [V((30, CHANS, CHANS), BF)] * 2
            + [V((56, CHANS, TILE), BF)] + [V(hid, F32)] * 6 + [V((4 * CHANS, NT * TILE), BF)] * 3
            + [V((NT + 4, CHANS, TILE), BF)] * 3 + [V((31, 4, CHANS, TILE), BF)] + [V((32, CHANS, TILE), F32)] * 2
            + [D((7,)), D((32,)), D((56,)), D((32,)), D((2, 32)), D((2, 32))],
            compiler_params=pltpu.CompilerParams(vmem_limit_bytes=60 * 2**20, has_side_effects=True, collective_id=0),
        )(x_t, *weights)
        return jnp.swapaxes(h, 1, 2), jnp.swapaxes(skip, 1, 2)

    return jax.shard_map(local_stack, mesh=mesh, in_specs=(seq_spec, P(), P(), P(), P(), P(), P()), out_specs=(seq_spec, seq_spec), check_vma=False)
```

time: 101 us -> 83.4 us (0.83)
  the two profiles are of different devices: /device:TPU:121 before, /device:TPU:43 now
where the time goes in v2:
time: 83.4 us; the launch traced here: 83.3 us
  Pallas kernels  79.3 us (95%)
  local copies, waits for them, and re-layouts  3.37 us (4%)
    pallas_call x1, Pallas kernels, local_stack(): pl.pallas_call(kernel, out_shape=[out, out], in_specs=[pl.BlockSpec(memor...  79.3 us
    unnamed x4, local copies, waits for them, and re-layouts  3.37 us

profile of v2, /device:TPU:43, one launch (start us, length us, event | category | flops | bytes accessed | tf_op | source)
XLA Modules:
  0.0 83.3 jit_solution(9706309923089403458)
XLA Ops:
  0.6 79.3 %shard_map.86 = (f32[32,64,128]{2,1,0:T(8,128)}, f32[32,64,128]{2,1,0:T(8,128)}) custom-call(bf16[32,64,128]{2,1,0:T(8,128)(2,1)} %bitcast.5, bf16[3,10,64,64]{3,2,1,0:T(8,128)(2,1)} %wf0.1, bf16[3,10,64,64]{3,2,1,0:T(8,128)(2,1)} %wf1.1, bf16[3,10,64,64]{3,2,1,0:T(8,128)(2,1)} %wg0.1, bf16[3,10,64,64]{3,2,1,0:T(8,128)(2,1)} %wg1.1, ...), custom_call_target="tpu_custom_call" | custom-call | tf_op jit(solution)/shard_map/pallas_call | solution.py:287
  79.9 0.0 copy-start
  79.9 2.4 %copy.11 = f32[32,128,64]{1,2,0:T(8,128)} copy(f32[32,128,64]{1,2,0:T(8,128)} %bitcast.4) | data formatting | bytes 2097152
  82.3 0.0 copy-done
  82.3 1.0 %copy.12 = f32[32,128,64]{1,2,0:T(8,128)} copy(f32[32,128,64]{1,2,0:T(8,128)S(1)} %bitcast.3) | data formatting | bytes 2097152
Async XLA Ops:
  79.9 2.4 %copy-start = (f32[32,64,128]{2,1,0:T(8,128)S(1)}, f32[32,64,128]{2,1,0:T(8,128)}, u32[]{:S(2)}) copy-start(f32[32,64,128]{2,1,0:T(8,128)} %get-tuple-element.5) | copy-start | bytes 3145732

commit v3 on v2

--- a/solution.py
+++ b/solution.py
@@ -83,8 +83,16 @@
             middle(t - LAG1)
 
 
-def shift_of(s):
-    return lax.rem((s % 8) // 2 + s % 2, 4)
+def low(v, n):
+    return lax.bitwise_and(v, jnp.int32(n - 1))
+
+
+def high(v, bits):
+    return lax.shift_right_logical(v, jnp.int32(bits))
+
+
+def shift_of(k):
+    return low(high(k, 1) + low(k, 2), 4)
 
 
 def kernel(x_hbm, wf0, wf1, wg0, wg1, wres, wskip, hout, sout, x, w0, w1, w2, w3, w4, w5, w1t, wrt, wst, xbuf,
@@ -95,75 +103,86 @@
     for load in loads:
         load.start()
     hi, k = lax.axis_index("seq_hi"), lax.axis_index("seq")
-    z, row = hi // 4, hi % 4
+    z, row = high(hi, 2), low(hi, 4)
     me = row * 8 + k
-    first = 4 * z + shift_of(me)
+    shift = shift_of(k)
+    first = 4 * z + shift
+    mine = (3 + row - shift) * NT + k
+    keeps = row >= shift
 
     def device(h, m):
         return {"seq_hi": h, "seq": m}
 
     def place(s):
-        e = lax.rem(hi - shift_of(s) + 16, 16)
-        return e // 4, e % 4
+        off = shift_of(low(s, 8))
+        e = low(hi - off, 16)
+        q, c = high(e, 2), low(e, 4)
+        return q, c, jnp.logical_and(c >= 1, jnp.logical_or(q != 3, hi < off))
 
     def own_copy(s):
-        q, c = place(s)
+        q, c, _ = place(s)
         slot = (3 + c) * NT + k
-        go = jnp.logical_or(q != z, s != me)
-        return go, pltpu.make_async_remote_copy(
+        return pltpu.make_async_remote_copy(
             src_ref=x.at[s], dst_ref=xbuf.at[slot], send_sem=in_send.at[s], recv_sem=in_recv.at[slot],
-            device_id=device(q * 4 + s // 8, s % 8), device_id_type=MESH)
+            device_id=device(q * 4 + high(s, 3), low(s, 8)), device_id_type=MESH)
+
+    def owns(s):
+        return jnp.logical_or(s != me, jnp.logical_not(keeps))
 
     def halo_copy(s):
-        q, c = place(s)
-        nxt = lax.rem(q + 1, 4)
-        slot = lax.rem(c + 3, 4) * NT + k
-        go = jnp.logical_and(c >= 1, jnp.logical_or(q != 3, hi < shift_of(s)))
-        go = jnp.logical_and(go, jnp.logical_or(nxt != z, s != me))
-        return go, pltpu.make_async_remote_copy(
+        q, c, _ = place(s)
+        slot = (c - 1) * NT + k
+        return pltpu.make_async_remote_copy(
             src_ref=x.at[s], dst_ref=xbuf.at[slot], send_sem=halo_send.at[s], recv_sem=in_recv.at[slot],
-            device_id=device(nxt * 4 + s // 8, s % 8), device_id_type=MESH)
-
-    def source(slot):
-        g = first - 3 + slot // NT
-        src = lax.rem(g + 16, 16)
-        return g, src, jnp.logical_and(g >= 0, jnp.logical_or(src != hi, slot % NT != k))
+            device_id=device(low(q + 1, 4) * 4 + high(s, 3), low(s, 8)), device_id_type=MESH)
+
+    def halos(s):
+        return jnp.logical_and(place(s)[2], jnp.logical_or(s != me, keeps))
 
     def out_copy(i, src, dst, t):
-        g = lax.rem(first + t // NT, 16)
+        g = low(first + high(t, 3), 16)
         return pltpu.make_async_remote_copy(
             src_ref=src.at[t], dst_ref=dst.at[me], send_sem=out_send.at[i, t], recv_sem=out_recv.at[i, me],
-            device_id=device(g, t % NT), device_id_type=MESH)
-
-    def out_goes(t):
-        return jnp.logical_or(lax.rem(first + t // NT, 16) != hi, t % NT != k)
+            device_id=device(g, low(t, NT)), device_id_type=MESH)
+
+    def leaves(t):
+        return t + 3 * NT != mine
 
     def order(o):
-        return lax.rem(me + 5 * o, 32)
+        return low(me + 7 * o, 32)
 
     barrier = pltpu.get_barrier_semaphore()
 
-    def greet(slot, c):
-        g, src, remote = source(slot)
-
-        @pl.when(remote)
-        def _():
-            pl.semaphore_signal(barrier, inc=1, device_id=device(src, slot % NT), device_id_type=MESH)
-        return c
-
-    lax.fori_loop(0, 56, greet, 0)
-    peers = lax.fori_loop(0, 32, lambda s, n: n + own_copy(s)[0].astype(jnp.int32) + halo_copy(s)[0].astype(jnp.int32), jnp.int32(0))
+    def greet(i, c):
+        for kk in range(7):
+            g = first - 3 + kk
+
+            @pl.when(jnp.logical_and(g >= 0, kk * NT + i != mine))
+            def _():
+                pl.semaphore_signal(barrier, inc=1, device_id=device(low(g, 16), i), device_id_type=MESH)
+        return c
+
+    lax.fori_loop(0, NT, greet, 0)
+    peers = jnp.int32(31)
+    for m in range(NT):
+        peers = peers + 4 * place(jnp.int32(m))[2].astype(jnp.int32)
     loads[0].wait()
     pl.semaphore_wait(barrier, peers)
 
     def start_halo(o, c):
-        go, copy = halo_copy(order(o))
-        pl.when(go)(copy.start)
+        s = order(o)
+
+        @pl.when(halos(s))
+        def _():
+            halo_copy(s).start()
         return c
 
     def start_own(o, c):
-        go, copy = own_copy(order(o))
-        pl.when(go)(copy.start)
+        s = order(o)
+
+        @pl.when(owns(s))
+        def _():
+            own_copy(s).start()
         return c
 
     lax.fori_loop(0, 32, start_halo, 0)
@@ -176,8 +195,8 @@
         for r in range(3):
             layer = r * CYCLE + c
             top = jnp.concatenate([w1[r, c], w3[r, c]], 1)
-            low = jnp.concatenate([w0[r, c], w2[r, c]], 1)
-            w1t[layer] = jnp.concatenate([top, low], 0).astype(F32).T.astype(BF)
+            bottom = jnp.concatenate([w0[r, c], w2[r, c]], 1)
+            w1t[layer] = jnp.concatenate([top, bottom], 0).astype(F32).T.astype(BF)
             last = jnp.concatenate([w4[r, c], w5[r, c]], 1).astype(F32).T.astype(BF)
             wrt[layer] = last[:CHANS]
             wst[layer] = last[CHANS:]
@@ -187,19 +206,25 @@
 
     lane = lax.broadcasted_iota(jnp.int32, (CHANS, TILE), 1)
     hist[...] = jnp.zeros_like(hist)
-    xbuf[(3 + row - shift_of(me)) * NT + k] = x[me]
+    xbuf[mine] = x[me]
     for kk in range(3):
         @pl.when(first - 3 + kk < 0)
         def _():
             xbuf[kk * NT : (kk + 1) * NT] = jnp.zeros((NT, CHANS, TILE), BF)
 
-    def wait_slot(slot, c):
-        @pl.when(source(slot)[2])
-        def _():
-            pltpu.make_async_copy(xbuf.at[slot], xbuf.at[slot], in_recv.at[slot]).wait()
-        return c
-
-    lax.fori_loop(0, 3 * NT, wait_slot, 0)
+    def wait_chunk(kk):
+        @pl.when(first - 3 + kk >= 0)
+        def _():
+            def wait_slot(slot, c):
+                @pl.when(slot != mine)
+                def _():
+                    pltpu.make_async_copy(xbuf.at[slot], xbuf.at[slot], in_recv.at[slot]).wait()
+                return c
+
+            lax.fori_loop(kk * NT, kk * NT + NT, wait_slot, 0)
+
+    for kk in range(3):
+        wait_chunk(kk)
 
     def macro(s):
         @pl.when(s >= 3)
@@ -222,9 +247,8 @@
 
         @pl.when(jnp.logical_and(s >= 1, s <= 4))
         def _():
-            base = (s + 2) * NT
-            lax.fori_loop(base, base + NT, wait_slot, 0)
-            hA[...] = xbuf[pl.ds(base, NT)].astype(F32)
+            wait_chunk(s + 2)
+            hA[...] = xbuf[pl.ds((s + 2) * NT, NT)].astype(F32)
             sA[...] = jnp.zeros_like(sA)
 
         reps = [0, jnp.minimum(s, 1), jnp.minimum(s, 2)]
@@ -238,9 +262,9 @@
             sstage[pl.ds(base, NT)] = sC[...]
 
             def send(o, c):
-                t = base + lax.rem(3 * o + k, NT)
-
-                @pl.when(out_goes(t))
+                t = base + low(3 * o + k, NT)
+
+                @pl.when(leaves(t))
                 def _():
                     out_copy(0, hstage, hout, t).start()
                     out_copy(1, sstage, sout, t).start()
@@ -250,24 +274,30 @@
 
     lax.fori_loop(0, 7, lambda s, c: (macro(s), c)[1], 0)
 
-    keeps = row >= shift_of(me)
-
     @pl.when(keeps)
     def _():
-        t = (row - shift_of(me)) * NT + k
-        hout[me] = hstage[t]
-        sout[me] = sstage[t]
-
-    def drain(s, c):
-        for go, copy in (own_copy(s), halo_copy(s)):
-            pl.when(go)(copy.wait_send)
-
-        @pl.when(out_goes(s))
+        hout[me] = hstage[mine - 3 * NT]
+        sout[me] = sstage[mine - 3 * NT]
+
+    def drain_sends(s, c):
+        @pl.when(owns(s))
+        def _():
+            own_copy(s).wait_send()
+
+        @pl.when(halos(s))
+        def _():
+            halo_copy(s).wait_send()
+
+        @pl.when(leaves(s))
         def _():
             out_copy(0, hstage, hout, s).wait_send()
             out_copy(1, sstage, sout, s).wait_send()
-
-        @pl.when(own_copy(s)[0])
+        return c
+
+    lax.fori_loop(0, 32, drain_sends, 0)
+
+    def drain(s, c):
+        @pl.when(owns(s))
         def _():
             pltpu.make_async_copy(hout.at[s], hout.at[s], out_recv.at[0, s]).wait()
             pltpu.make_async_copy(sout.at[s], sout.at[s], out_recv.at[1, s]).wait()
@@ -287,15 +317,15 @@
         h, skip = pl.pallas_call(
             kernel,
             out_shape=[out, out],
-            in_specs=[pl.BlockSpec(memory_space=pl.ANY)] * 7,
+            in_specs=[pl.BlockSpec(memory_space=pltpu.HBM)] * 7,
             out_specs=[pl.BlockSpec(memory_space=V)] * 2,
             scratch_shapes=[V((32, CHANS, TILE), BF)] + [V((3, CYCLE, CHANS, CHANS), BF)] * 6
             + [V((30, 2 * CHANS, 2 * CHANS), BF)] + [V((30, CHANS, CHANS), BF)] * 2
             + [V((56, CHANS, TILE), BF)] + [V(hid, F32)] * 6 + [V((4 * CHANS, NT * TILE), BF)] * 3
             + [V((NT + 4, CHANS, TILE), BF)] * 3 + [V((31, 4, CHANS, TILE), BF)] + [V((32, CHANS, TILE), F32)] * 2
             + [D((7,)), D((32,)), D((56,)), D((32,)), D((2, 32)), D((2, 32))],
-            compiler_params=pltpu.CompilerParams(vmem_limit_bytes=60 * 2**20, has_side_effects=True, collective_id=0),
-        )(x_t, *weights)
+            compiler_params=pltpu.CompilerParams(vmem_limit_bytes=24 * 2**20, has_side_effects=True, collective_id=0),
+        )(*[pltpu.with_memory_space_constraint(a, pltpu.HBM) for a in (x_t, *weights)])
         return jnp.swapaxes(h, 1, 2), jnp.swapaxes(skip, 1, 2)
 
     return jax.shard_map(local_stack, mesh=mesh, in_specs=(seq_spec, P(), P(), P(), P(), P(), P()), out_specs=(seq_spec, seq_spec), check_vma=False)

time: 83.4 us -> 76.9 us (0.922)
  the two profiles are of different devices: /device:TPU:43 before, /device:TPU:35 now
where the time goes in v3:
time: 76.9 us; the launch traced here: 76.8 us
  Pallas kernels  74.2 us (96%)
  local copies, waits for them, and re-layouts  1.94 us (3%)
    pallas_call x1, Pallas kernels, local_stack(): pl.pallas_call(kernel, out_shape=[out, out], in_specs=[pl.BlockSpec(memor...  74.2 us
    unnamed x2, local copies, waits for them, and re-layouts  1.94 us

profile of v3, /device:TPU:35, one launch (start us, length us, event | category | flops | bytes accessed | tf_op | source)
XLA Modules:
  0.0 76.8 jit_solution(2427801998269494775)
XLA Ops:
  0.6 74.2 %shard_map.86 = (f32[32,64,128]{2,1,0:T(8,128)S(1)}, f32[32,64,128]{2,1,0:T(8,128)S(1)}) custom-call(bf16[32,64,128]{2,1,0:T(8,128)(2,1)} %bitcast.5, bf16[3,10,64,64]{3,2,1,0:T(8,128)(2,1)} %wf0.1, bf16[3,10,64,64]{3,2,1,0:T(8,128)(2,1)} %wf1.1, bf16[3,10,64,64]{3,2,1,0:T(8,128)(2,1)} %wg0.1, bf16[3,10,64,64]{3,2,1,0:T(8,128)(2,1)} %wg1.1, ...), custom_call_target="tpu_custom_call" | custom-call | tf_op jit(solution)/shard_map/pallas_call | solution.py:317
  74.9 1.0 %copy.11 = f32[32,128,64]{1,2,0:T(8,128)} copy(f32[32,128,64]{1,2,0:T(8,128)S(1)} %bitcast.4) | data formatting | bytes 2097152
  75.8 1.0 %copy.12 = f32[32,128,64]{1,2,0:T(8,128)} copy(f32[32,128,64]{1,2,0:T(8,128)S(1)} %bitcast.3) | data formatting | bytes 2097152

commit v4 on v3

--- a/solution.py
+++ b/solution.py
@@ -91,8 +91,9 @@
     return lax.shift_right_logical(v, jnp.int32(bits))
 
 
-def shift_of(k):
-    return low(high(k, 1) + low(k, 2), 4)
+def shift_of(s):
+    r, x, core = high(s, 3), high(low(s, 8), 1), low(s, 2)
+    return low(x + r + 2 * core, 4) - 1 - low(r, 2)
 
 
 def kernel(x_hbm, wf0, wf1, wg0, wg1, wres, wskip, hout, sout, x, w0, w1, w2, w3, w4, w5, w1t, wrt, wst, xbuf,
@@ -105,19 +106,23 @@
     hi, k = lax.axis_index("seq_hi"), lax.axis_index("seq")
     z, row = high(hi, 2), low(hi, 4)
     me = row * 8 + k
-    shift = shift_of(k)
-    first = 4 * z + shift
-    mine = (3 + row - shift) * NT + k
-    keeps = row >= shift
+    first = low(4 * z + shift_of(me), 16)
 
     def device(h, m):
         return {"seq_hi": h, "seq": m}
 
     def place(s):
-        off = shift_of(low(s, 8))
+        return dealt(shift_of(s))
+
+    def dealt(off):
         e = low(hi - off, 16)
         q, c = high(e, 2), low(e, 4)
-        return q, c, jnp.logical_and(c >= 1, jnp.logical_or(q != 3, hi < off))
+        return q, c, jnp.logical_and(c >= 1, low(4 * q + 4 + off, 16) + c >= 4)
+
+    my_q, my_c, my_halo = place(me)
+    keeps = my_q == z
+    reuses = jnp.logical_and(my_halo, low(my_q + 1, 4) == z)
+    mine = jnp.where(keeps, (3 + my_c) * NT + k, jnp.where(reuses, (my_c - 1) * NT + k, -1))
 
     def own_copy(s):
         q, c, _ = place(s)
@@ -137,7 +142,7 @@
             device_id=device(low(q + 1, 4) * 4 + high(s, 3), low(s, 8)), device_id_type=MESH)
 
     def halos(s):
-        return jnp.logical_and(place(s)[2], jnp.logical_or(s != me, keeps))
+        return jnp.logical_and(place(s)[2], jnp.logical_or(s != me, jnp.logical_not(reuses)))
 
     def out_copy(i, src, dst, t):
         g = low(first + high(t, 3), 16)
@@ -148,9 +153,6 @@
     def leaves(t):
         return t + 3 * NT != mine
 
-    def order(o):
-        return low(me + 7 * o, 32)
-
     barrier = pltpu.get_barrier_semaphore()
 
     def greet(i, c):
@@ -163,30 +165,47 @@
         return c
 
     lax.fori_loop(0, NT, greet, 0)
-    peers = jnp.int32(31)
-    for m in range(NT):
-        peers = peers + 4 * place(jnp.int32(m))[2].astype(jnp.int32)
+    peers = 32 - keeps.astype(jnp.int32) - reuses.astype(jnp.int32)
+    for m in range(4):
+        for parity in range(2):
+            peers = peers + 4 * dealt(jnp.int32(m - 1 - parity))[2].astype(jnp.int32)
     loads[0].wait()
     pl.semaphore_wait(barrier, peers)
 
-    def start_halo(o, c):
-        s = order(o)
-
-        @pl.when(halos(s))
-        def _():
-            halo_copy(s).start()
-        return c
-
-    def start_own(o, c):
-        s = order(o)
-
+    def spread(body):
+        core = low(k, 2)
+        start = row + high(k, 1) + 2 * core
+
+        def turn(i, carry):
+            m = low(start + i, 4)
+            for parity in range(2):
+                q, c, halo = dealt(m - 1 - low(row + parity, 2))
+                for j in range(4):
+                    r, co = low(row + parity + 2 * (j // 2), 4), low(core + j, 2)
+                    s = r * 8 + 2 * low(m - r - 2 * co, 4) + co
+                    body(s, q, c, halo, r)
+            return carry
+
+        lax.fori_loop(0, 4, turn, 0)
+
+    def start_halo(s, q, c, halo, r):
+        @pl.when(jnp.logical_and(halo, jnp.logical_or(s != me, jnp.logical_not(reuses))))
+        def _():
+            slot = (c - 1) * NT + k
+            pltpu.make_async_remote_copy(
+                src_ref=x.at[s], dst_ref=xbuf.at[slot], send_sem=halo_send.at[s], recv_sem=in_recv.at[slot],
+                device_id=device(low(q + 1, 4) * 4 + r, low(s, 8)), device_id_type=MESH).start()
+
+    def start_own(s, q, c, halo, r):
         @pl.when(owns(s))
         def _():
-            own_copy(s).start()
-        return c
-
-    lax.fori_loop(0, 32, start_halo, 0)
-    lax.fori_loop(0, 32, start_own, 0)
+            slot = (3 + c) * NT + k
+            pltpu.make_async_remote_copy(
+                src_ref=x.at[s], dst_ref=xbuf.at[slot], send_sem=in_send.at[s], recv_sem=in_recv.at[slot],
+                device_id=device(q * 4 + r, low(s, 8)), device_id_type=MESH).start()
+
+    spread(start_halo)
+    spread(start_own)
 
     for load in loads[1:]:
         load.wait()
@@ -206,7 +225,11 @@
 
     lane = lax.broadcasted_iota(jnp.int32, (CHANS, TILE), 1)
     hist[...] = jnp.zeros_like(hist)
-    xbuf[mine] = x[me]
+
+    @pl.when(mine >= 0)
+    def _():
+        xbuf[jnp.maximum(mine, 0)] = x[me]
+
     for kk in range(3):
         @pl.when(first - 3 + kk < 0)
         def _():
@@ -276,8 +299,8 @@
 
     @pl.when(keeps)
     def _():
-        hout[me] = hstage[mine - 3 * NT]
-        sout[me] = sstage[mine - 3 * NT]
+        hout[me] = hstage[jnp.maximum(mine - 3 * NT, 0)]
+        sout[me] = sstage[jnp.maximum(mine - 3 * NT, 0)]
 
     def drain_sends(s, c):
         @pl.when(owns(s))

time: 76.9 us -> 74.1 us (0.964)
  the two profiles are of different devices: /device:TPU:35 before, /device:TPU:1 now
where the time goes in v4:
time: 74.1 us; the launch traced here: 74 us
  Pallas kernels  71.4 us (96%)
  local copies, waits for them, and re-layouts  1.94 us (3%)
    pallas_call x1, Pallas kernels, local_stack(): pl.pallas_call(kernel, out_shape=[out, out], in_specs=[pl.BlockSpec(memor...  71.4 us
    unnamed x2, local copies, waits for them, and re-layouts  1.94 us

profile of v4, /device:TPU:1, one launch (start us, length us, event | category | flops | bytes accessed | tf_op | source)
XLA Modules:
  0.0 74.0 jit_solution(8611388499823164110)
XLA Ops:
  0.6 71.4 %shard_map.86 = (f32[32,64,128]{2,1,0:T(8,128)S(1)}, f32[32,64,128]{2,1,0:T(8,128)S(1)}) custom-call(bf16[32,64,128]{2,1,0:T(8,128)(2,1)} %bitcast.5, bf16[3,10,64,64]{3,2,1,0:T(8,128)(2,1)} %wf0.1, bf16[3,10,64,64]{3,2,1,0:T(8,128)(2,1)} %wf1.1, bf16[3,10,64,64]{3,2,1,0:T(8,128)(2,1)} %wg0.1, bf16[3,10,64,64]{3,2,1,0:T(8,128)(2,1)} %wg1.1, ...), custom_call_target="tpu_custom_call" | custom-call | tf_op jit(solution)/shard_map/pallas_call | solution.py:340
  72.0 1.0 %copy.11 = f32[32,128,64]{1,2,0:T(8,128)} copy(f32[32,128,64]{1,2,0:T(8,128)S(1)} %bitcast.4) | data formatting | bytes 2097152
  73.0 1.0 %copy.12 = f32[32,128,64]{1,2,0:T(8,128)} copy(f32[32,128,64]{1,2,0:T(8,128)S(1)} %bitcast.3) | data formatting | bytes 2097152

commit v5 on v4

--- a/solution.py
+++ b/solution.py
@@ -93,7 +93,11 @@
 
 def shift_of(s):
     r, x, core = high(s, 3), high(low(s, 8), 1), low(s, 2)
-    return low(x + r + 2 * core, 4) - 1 - low(r, 2)
+    return dealt_from(low(x + r + 2 * core, 4))
+
+
+def dealt_from(m):
+    return jnp.where(m == 0, 0, jnp.where(m == 1, -1, jnp.where(m == 2, 1, 0)))
 
 
 def kernel(x_hbm, wf0, wf1, wg0, wg1, wres, wskip, hout, sout, x, w0, w1, w2, w3, w4, w5, w1t, wrt, wst, xbuf,
@@ -168,7 +172,7 @@
     peers = 32 - keeps.astype(jnp.int32) - reuses.astype(jnp.int32)
     for m in range(4):
         for parity in range(2):
-            peers = peers + 4 * dealt(jnp.int32(m - 1 - parity))[2].astype(jnp.int32)
+            peers = peers + 4 * dealt(dealt_from(jnp.int32(m)))[2].astype(jnp.int32)
     loads[0].wait()
     pl.semaphore_wait(barrier, peers)
 
@@ -179,7 +183,7 @@
         def turn(i, carry):
             m = low(start + i, 4)
             for parity in range(2):
-                q, c, halo = dealt(m - 1 - low(row + parity, 2))
+                q, c, halo = dealt(dealt_from(m))
                 for j in range(4):
                     r, co = low(row + parity + 2 * (j // 2), 4), low(core + j, 2)
                     s = r * 8 + 2 * low(m - r - 2 * co, 4) + co
@@ -285,7 +289,7 @@
             sstage[pl.ds(base, NT)] = sC[...]
 
             def send(o, c):
-                t = base + low(3 * o + k, NT)
+                t = base + low(5 * o + k, NT)
 
                 @pl.when(leaves(t))
                 def _():

time: 74.1 us -> 70.7 us (0.954)
  Pallas kernels: 71.4 us -> 68 us
    pallas_call x1, Pallas kernels: 71.4 us -> 68 us  [local_stack(): pl.pallas_call(kernel, out_shape=[out, out], in_specs=[pl.BlockSpec(memor...]
where the time goes in v5:
time: 70.7 us; the launch traced here: 70.6 us
  Pallas kernels  68 us (96%)
  local copies, waits for them, and re-layouts  1.94 us (3%)
    pallas_call x1, Pallas kernels, local_stack(): pl.pallas_call(kernel, out_shape=[out, out], in_specs=[pl.BlockSpec(memor...  68 us
    unnamed x2, local copies, waits for them, and re-layouts  1.94 us

profile of v5, /device:TPU:1, one launch (start us, length us, event | category | flops | bytes accessed | tf_op | source)
XLA Modules:
  0.0 70.6 jit_solution(18401111891658440391)
XLA Ops:
  0.6 68.0 %shard_map.86 = (f32[32,64,128]{2,1,0:T(8,128)S(1)}, f32[32,64,128]{2,1,0:T(8,128)S(1)}) custom-call(bf16[32,64,128]{2,1,0:T(8,128)(2,1)} %bitcast.5, bf16[3,10,64,64]{3,2,1,0:T(8,128)(2,1)} %wf0.1, bf16[3,10,64,64]{3,2,1,0:T(8,128)(2,1)} %wf1.1, bf16[3,10,64,64]{3,2,1,0:T(8,128)(2,1)} %wg0.1, bf16[3,10,64,64]{3,2,1,0:T(8,128)(2,1)} %wg1.1, ...), custom_call_target="tpu_custom_call" | custom-call | tf_op jit(solution)/shard_map/pallas_call | solution.py:344
  68.7 1.0 %copy.11 = f32[32,128,64]{1,2,0:T(8,128)} copy(f32[32,128,64]{1,2,0:T(8,128)S(1)} %bitcast.4) | data formatting | bytes 2097152
  69.7 1.0 %copy.12 = f32[32,128,64]{1,2,0:T(8,128)} copy(f32[32,128,64]{1,2,0:T(8,128)S(1)} %bitcast.3) | data formatting | bytes 2097152

commit v6 on v5

--- a/solution.py
+++ b/solution.py
@@ -333,6 +333,15 @@
     lax.fori_loop(0, 32, drain, 0)
 
 
+def leave(h, skip, h_out, skip_out, sems):
+    copies = [pltpu.make_async_copy(a.at[pl.ds(16 * i, 16)], b.at[pl.ds(16 * i, 16)], sems.at[i, n])
+              for n, (a, b) in enumerate(((h, h_out), (skip, skip_out))) for i in range(2)]
+    for copy in copies:
+        copy.start()
+    for copy in copies:
+        copy.wait()
+
+
 def solution(mesh):
     seq_spec = P("batch", SEQ_AXES, None)
 
@@ -353,6 +362,14 @@
             + [D((7,)), D((32,)), D((56,)), D((32,)), D((2, 32)), D((2, 32))],
             compiler_params=pltpu.CompilerParams(vmem_limit_bytes=24 * 2**20, has_side_effects=True, collective_id=0),
         )(*[pltpu.with_memory_space_constraint(a, pltpu.HBM) for a in (x_t, *weights)])
+        h, skip = pl.pallas_call(
+            leave,
+            out_shape=[out, out],
+            in_specs=[pl.BlockSpec(memory_space=V)] * 2,
+            out_specs=[pl.BlockSpec(memory_space=pltpu.HBM)] * 2,
+            scratch_shapes=[D((2, 2))],
+            compiler_params=pltpu.CompilerParams(vmem_limit_bytes=8 * 2**20),
+        )(h, skip)
         return jnp.swapaxes(h, 1, 2), jnp.swapaxes(skip, 1, 2)
 
     return jax.shard_map(local_stack, mesh=mesh, in_specs=(seq_spec, P(), P(), P(), P(), P(), P()), out_specs=(seq_spec, seq_spec), check_vma=False)

time: 70.7 us -> 70.1 us (level)
  local copies, waits for them, and re-layouts: 1.94 us -> 0 us
  Pallas kernels: 68 us -> 69.4 us
    unnamed x2 -> x0, local copies, waits for them, and re-layouts: 1.94 us -> none
    pallas_call x0 -> x1, Pallas kernels: none -> 1.35 us  [local_stack(): pl.pallas_call(leave, out_shape=[out, out], in_specs=[pl.BlockSpec(memory...]
where the time goes in v6:
time: 70.1 us; the launch traced here: 70 us
  Pallas kernels  69.4 us (99%)
    pallas_call x1, Pallas kernels, local_stack(): pl.pallas_call(kernel, out_shape=[out, out], in_specs=[pl.BlockSpec(memor...  68 us

profile of v6, /device:TPU:1, one launch (start us, length us, event | category | flops | bytes accessed | tf_op | source)
XLA Modules:
  0.0 70.0 jit_solution(11704481111979307003)
XLA Ops:
  0.6 68.0 %shard_map.86 = (f32[32,64,128]{2,1,0:T(8,128)S(1)}, f32[32,64,128]{2,1,0:T(8,128)S(1)}) custom-call(bf16[32,64,128]{2,1,0:T(8,128)(2,1)} %bitcast.3, bf16[3,10,64,64]{3,2,1,0:T(8,128)(2,1)} %wf0.1, bf16[3,10,64,64]{3,2,1,0:T(8,128)(2,1)} %wf1.1, bf16[3,10,64,64]{3,2,1,0:T(8,128)(2,1)} %wg0.1, bf16[3,10,64,64]{3,2,1,0:T(8,128)(2,1)} %wg1.1, ...), custom_call_target="tpu_custom_call" | custom-call | tf_op jit(solution)/shard_map/pallas_call | solution.py:353
  68.7 1.3 %shard_map.87 = (f32[32,64,128]{2,1,0:T(8,128)}, f32[32,64,128]{2,1,0:T(8,128)}) custom-call(f32[32,64,128]{2,1,0:T(8,128)S(1)} %get-tuple-element.6.h, f32[32,64,128]{2,1,0:T(8,128)S(1)} %get-tuple-element.7.skip), custom_call_target="tpu_custom_call" | custom-call | tf_op jit(solution)/shard_map/pallas_call | solution.py:365

commit v7 on v6

--- a/solution.py
+++ b/solution.py
@@ -228,7 +228,8 @@
     lax.fori_loop(0, CYCLE, prepare, 0)
 
     lane = lax.broadcasted_iota(jnp.int32, (CHANS, TILE), 1)
-    hist[...] = jnp.zeros_like(hist)
+    for ref in (hist, sA, sB, sC):
+        ref[...] = jnp.zeros_like(ref)
 
     @pl.when(mine >= 0)
     def _():
@@ -269,8 +270,6 @@
             hA[...] = xbuf[0:8].astype(F32)
             hB[...] = xbuf[8:16].astype(F32)
             hC[...] = xbuf[16:24].astype(F32)
-            for ref in (sA, sB, sC):
-                ref[...] = jnp.zeros_like(ref)
 
         @pl.when(jnp.logical_and(s >= 1, s <= 4))
         def _():
@@ -289,7 +288,7 @@
             sstage[pl.ds(base, NT)] = sC[...]
 
             def send(o, c):
-                t = base + low(5 * o + k, NT)
+                t = base + low(k + 2 * o + high(o, 2), NT)
 
                 @pl.when(leaves(t))
                 def _():

time: 70.1 us -> 71.6 us (1.021)
  Pallas kernels: 69.4 us -> 70.8 us
    pallas_call x1, Pallas kernels: 68 us -> 69.5 us  [local_stack(): pl.pallas_call(kernel, out_shape=[out, out], in_specs=[pl.BlockSpec(memor...]
where the time goes in v7:
time: 71.6 us; the launch traced here: 71.4 us
  Pallas kernels  70.8 us (99%)
    pallas_call x1, Pallas kernels, local_stack(): pl.pallas_call(kernel, out_shape=[out, out], in_specs=[pl.BlockSpec(memor...  69.5 us

profile of v7, /device:TPU:1, one launch (start us, length us, event | category | flops | bytes accessed | tf_op | source)
XLA Modules:
  0.0 71.4 jit_solution(5732363624263286992)
XLA Ops:
  0.6 69.5 %shard_map.86 = (f32[32,64,128]{2,1,0:T(8,128)S(1)}, f32[32,64,128]{2,1,0:T(8,128)S(1)}) custom-call(bf16[32,64,128]{2,1,0:T(8,128)(2,1)} %bitcast.3, bf16[3,10,64,64]{3,2,1,0:T(8,128)(2,1)} %wf0.1, bf16[3,10,64,64]{3,2,1,0:T(8,128)(2,1)} %wf1.1, bf16[3,10,64,64]{3,2,1,0:T(8,128)(2,1)} %wg0.1, bf16[3,10,64,64]{3,2,1,0:T(8,128)(2,1)} %wg1.1, ...), custom_call_target="tpu_custom_call" | custom-call | tf_op jit(solution)/shard_map/pallas_call | solution.py:352
  70.1 1.3 %shard_map.87 = (f32[32,64,128]{2,1,0:T(8,128)}, f32[32,64,128]{2,1,0:T(8,128)}) custom-call(f32[32,64,128]{2,1,0:T(8,128)S(1)} %get-tuple-element.6.h, f32[32,64,128]{2,1,0:T(8,128)S(1)} %get-tuple-element.7.skip), custom_call_target="tpu_custom_call" | custom-call | tf_op jit(solution)/shard_map/pallas_call | solution.py:364
